TPU v7x, 32 devices: a whole 2x2x4 slice. The times are simulated.
32 devices in a mesh: dp: 8 (over z, y), section: 2 (over core), tensor: 2 (over x).
Axes of the slice: x: 2, y: 2, z: 4, core: 2. Of those that a mesh axis runs over, the one named last changes fastest.
Arguments:
- tower_input: bfloat16 [2, 1536, 1024], P('section', 'dp'), may hold values from -8 to 8
- up_weight: bfloat16 [2, 1024, 4096], P('section', None, 'tensor'), may hold values from -0.1875 to 0.1875
- down_weight: bfloat16 [2, 4096, 1024], P('section', 'tensor'), may hold values from -0.09375 to 0.09375
- pair: int32 [1536], P('dp'), may hold values from 0 to 1535, each once
- scale: float32 [1], replicated, may hold values from 4 to 16
- bias: float32 [1], replicated, may hold values from -4 to -1
Outputs:
- loss: float32 [1], replicated
- slide_grad: float32 [1536, 1024], P(('dp', 'section', 'tensor'))
- report_grad: float32 [1536, 1024], P(('dp', 'section', 'tensor'))
Inputs may be any that keep to these rules, and one draw needn't show every extreme that they name: `pair`: each report index appears exactly once.
All inputs are finite; a program needn't handle non-finite values.
Results may differ from a plain program's by a relative error of at most 0.00036.
Values may be sent and summed in bfloat16 or wider, within the bound.
A program may use at most 128 MiB of HBM per device.

v0:
```python
import jax
import jax.numpy as jnp
from jax import lax
from jax.sharding import PartitionSpec as P


def score_block(slides_all, block, pair, columns, scale_value, bias_value):
    logits = (
        scale_value
        * lax.dot_general(
            slides_all, block, (((1,), (1,)), ((), ())), preferred_element_type=jnp.float32
        )
        + bias_value
    )
    sign = jnp.where(pair[:, None] == columns[None, :], 1.0, -1.0).astype(jnp.float32)
    loss_part = jnp.sum(jnp.logaddexp(jnp.float32(0.0), -sign * logits))
    weight = (-scale_value * sign * jax.nn.sigmoid(-sign * logits)).astype(jnp.bfloat16)
    slide_part = jnp.dot(weight, block, preferred_element_type=jnp.float32)
    report_part = lax.dot_general(
        weight, slides_all, (((0,), (0,)), ((), ())), preferred_element_type=jnp.float32
    )
    return (loss_part, slide_part, report_part)


def local(tower_input, up_weight, down_weight, pair, scale, bias):
    n_section = lax.axis_size("section")
    n_tensor = lax.axis_size("tensor")
    n_cycle = lax.axis_size("dp")
    group = n_section * n_tensor
    inputs = tower_input[0]
    width = inputs.shape[1]
    quarter = inputs.shape[0] // group
    hidden = jax.nn.gelu(jnp.dot(inputs, up_weight[0], preferred_element_type=jnp.float32)).astype(
        jnp.bfloat16
    )
    partial_value = jnp.dot(hidden, down_weight[0], preferred_element_type=jnp.float32)
    partial_value = partial_value.reshape(n_section, n_tensor, quarter, width)
    summed = lax.psum_scatter(partial_value, "tensor", scatter_dimension=1, tiled=True)
    local_in = lax.dynamic_slice_in_dim(
        inputs.reshape(n_section, n_tensor, quarter, width), lax.axis_index("tensor"), 1, 1
    )
    raw = (summed + local_in.astype(jnp.float32)).reshape(n_section, quarter, width)
    norms = lax.rsqrt(jnp.sum(raw * raw, axis=-1, keepdims=True) + 1e-06)
    embedded = (raw * norms).astype(jnp.bfloat16)
    both = lax.all_to_all(embedded, "section", split_axis=0, concat_axis=0, tiled=True)
    slides_all = lax.all_gather(both[0], ("section", "tensor"), axis=0, tiled=True)
    reports_own = both[1]
    group_rank = lax.axis_index("section") * n_tensor + lax.axis_index("tensor")
    scale_value = scale[0]
    bias_value = bias[0]
    total = n_cycle * group * quarter
    reports_group = lax.all_gather(reports_own, "dp", axis=0, tiled=True)
    position = jnp.arange(n_cycle * quarter, dtype=jnp.int32)
    columns = (position // quarter * group + group_rank) * quarter + position % quarter
    rows_half = slides_all.shape[0] // 2
    loss_top, slide_top, report_top = score_block(
        slides_all[:rows_half], reports_group, pair[:rows_half], columns, scale_value, bias_value
    )
    loss_bottom, slide_bottom, report_bottom = score_block(
        slides_all[rows_half:], reports_group, pair[rows_half:], columns, scale_value, bias_value
    )
    loss_sum = loss_top + loss_bottom
    slide_sum = jnp.concatenate([slide_top, slide_bottom], axis=0)
    report_grad = lax.psum_scatter(
        report_top + report_bottom, "dp", scatter_dimension=0, tiled=True
    )
    slide_grad = lax.psum_scatter(slide_sum, ("section", "tensor"), scatter_dimension=0, tiled=True)
    loss = lax.psum(loss_sum, ("dp", "section", "tensor")) / total
    return (loss.reshape(1), slide_grad, report_grad)


def solution(mesh):
    return jax.shard_map(
        local,
        mesh=mesh,
        in_specs=(
            P("section", "dp", None),
            P("section", None, "tensor"),
            P("section", "tensor", None),
            P("dp"),
            P(),
            P(),
        ),
        out_specs=(P(), P(("dp", "section", "tensor"), None), P(("dp", "section", "tensor"), None)),
        check_vma=False,
    )
```

profile of v0, /device:TPU:0, one launch (start us, length us, event | category | flops | bytes accessed | tf_op | source)
XLA Modules:
  0.0 206.1 jit_solution(15073694301376834896)
XLA Ops:
  7.2 0.0 all-reduce.3.cloned.1.call-start
  7.2 0.0 copy-start
  7.2 3.8 %fusion.13 = bf16[192,2048]{1,0:T(8,128)(2,1)S(1)} fusion(bf16[1,1024,2048]{2,1,0:T(8,128)(2,1)} %param.7, bf16[1,192,1024]{2,1,0:T(8,128)(2,1)} %param.6), kind=kOutput, calls=%fused_computation.12 | convolution fusion | flops 808845312 | bytes 5373952 | tf_op jit(solution)/shard_map/dot_general | solution.py:33
  11.0 0.0 copy-done
  11.0 0.0 copy-start.3
  11.0 0.0 copy-start.2
  11.1 0.0 copy-start.1
  11.1 1.9 fusion
  13.0 0.0 all-reduce.3.cloned.1.call-update
  13.0 0.0 reduce-scatter.4.cloned.1.call-start
  14.4 0.6 dynamic-slice
  15.0 0.0 copy-done.2
  15.0 0.1 fusion.49
  15.0 35.2 %all-reduce.3.cloned.1.call-done = f32[2,2,48,1024]{3,2,1,0:T(8,128)} async-done(((f32[2,2,48,1024]{3,2,1,0:T(8,128)}), f32[2,2,48,1024]{3,2,1,0:T(8,128)}) %all-reduce.3.cloned.1.call-update) | async-done | bytes 786448
  50.3 1.8 multiply_reduce_fusion
  52.0 1.7 multiply_convert_fusion
  53.8 3.9 %all_to_all.5 = bf16[2,48,1024]{2,1,0:T(8,128)(2,1)S(1)} all-to-all(bf16[2,48,1024]{2,1,0:T(8,128)(2,1)S(1)} %multiply_convert_fusion), channel_id=1, replica_groups=mesh['dp'=8,'section'=2,'tensor'=2] {'section'}, dimensions={0} | all-to-all | bytes 393216 | tf_op jit(solution)/shard_map/all_to_all | solution.py:45
  57.7 11.9 %all-gather = bf16[1,192,1024]{2,1,0:T(8,128)(2,1)S(1)} all-gather(bf16[1,48,1024]{2,1,0:T(8,128)(2,1)S(1)} %get-tuple-element.3), channel_id=2, replica_groups=mesh['dp'=8,'section'=2,'tensor'=2] {'section','tensor'}, dimensions={1}, use_global_device_ids=true | all-gather | bytes 491520 | tf_op jit(solution)/shard_map/all_gather | solution.py:46
  69.6 32.2 %all-gather.1 = bf16[1,384,1024]{2,1,0:T(8,128)(2,1)S(1)} all-gather(bf16[1,48,1024]{2,1,0:T(8,128)(2,1)S(1)} %get-tuple-element.4), channel_id=3, replica_groups=mesh['dp'=8,'section'=2,'tensor'=2] {'dp'}, dimensions={1}, use_global_device_ids=true | all-gather | bytes 884736 | tf_op jit(solution)/shard_map/all_gather | solution.py:52
  101.8 1.1 select_reduce_fusion.1
  102.9 0.3 fusion.22
  103.2 1.1 select_reduce_fusion
  104.3 0.3 fusion.20
  104.6 1.0 pad_maximum_fusion
  105.6 0.0 reduce-scatter.4.cloned.1.call-update
  105.6 0.0 reduce-scatter.6.cloned.1.call-start
  105.7 0.5 fusion.28
  106.1 1.6 convolution_add_fusion
  107.8 0.0 reduce-scatter.6.cloned.1.call-update
  109.0 38.5 %psum.7 = f32[]{:T(128)} all-reduce(f32[]{:T(128)S(6)} %add.114), channel_id=1, replica_groups=mesh['dp'=8,'section'=2,'tensor'=2] {'dp','section','tensor'}, use_global_device_ids=true, to_apply=%region_4.5 | all-reduce | flops 1 | bytes 8 | tf_op jit(solution)/shard_map/psum | solution.py:68
  148.1 0.0 reduce-scatter.4.cloned.1.call-done
  148.1 50.3 %reduce-scatter.6.cloned.1.call-done = f32[48,1024]{1,0:T(8,128)} async-done(((f32[384,1024]{1,0:T(8,128)}), f32[48,1024]{1,0:T(8,128)}) %reduce-scatter.6.cloned.1.call-update) | async-done | bytes 196624 | tf_op jit(solution)/shard_map/reduce_scatter | solution.py:64
  (5 shorter events, 0.0 us)
Async XLA Ops:
  7.2 43.1 %all-reduce.3.cloned.1.call-start = ((), (), s32[]{:S(2)}) async-start(), calls=%async_computation.5 | async-start | bytes 1572864
  7.2 3.8 %copy-start = (bf16[1,2048,1024]{2,1,0:T(8,128)(2,1)S(1)}, bf16[1,2048,1024]{2,1,0:T(8,128)(2,1)}, u32[]{:S(2)}) copy-start(bf16[1,2048,1024]{2,1,0:T(8,128)(2,1)} %param.8) | copy-start | bytes 12582916
  11.0 3.3 %copy-start.3 = (u32[32]{0:T(128)S(1)}, u32[32]{0:T(128)}, u32[]{:S(2)}) copy-start(u32[32]{0:T(128)} %constant.57) | copy-start | bytes 388
  11.0 3.9 %copy-start.2 = (s32[192]{0:T(256)S(1)}, s32[192]{0:T(256)}, u32[]{:S(2)}) copy-start(s32[192]{0:T(256)} %param.9) | copy-start | bytes 2308
  11.1 39.2 %copy-start.1 = (bf16[1,192,1024]{2,1,0:T(8,128)(2,1)S(1)}, bf16[1,192,1024]{2,1,0:T(8,128)(2,1)}, u32[]{:S(2)}) copy-start(bf16[1,192,1024]{2,1,0:T(8,128)(2,1)} %param.6) | copy-start | bytes 1179652
  13.0 135.1 %reduce-scatter.4.cloned.1.call-start = ((), (), s32[]{:S(2)}) async-start(), calls=%async_computation.3 | async-start | bytes 983040 | tf_op jit(solution)/shard_map/reduce_scatter | solution.py:67
  105.6 92.8 %reduce-scatter.6.cloned.1.call-start = ((), (), s32[]{:S(2)}) async-start(), calls=%async_computation.4 | async-start | bytes 1769472 | tf_op jit(solution)/shard_map/reduce_scatter | solution.py:64
Sparse Core Ops, SparseCore 0:
  13.1 37.0 all-reduce.2
  105.7 23.1 reduce-scatter.3
  132.9 65.4 reduce-scatter.5
where the time goes:
time: 207 us; the launch traced here: 206 us
  blocking collectives  86.5 us (42%)
  waiting for transfers between devices  85.6 us (41%)
  between operations  18.1 us (9%)
  matrix products  10.6 us (5%)
  other arithmetic  4.52 us (2%)
    reduce_scatter x1, waiting for transfers between devices, local(): lax.psum_scatter(report_top + report_bottom, 'dp', scatter_dimension=0, t...  50.3 us
    psum x1, blocking collectives, local(): loss = lax.psum(loss_sum, ('dp', 'section', 'tensor')) / total  38.5 us
    unnamed x4, waiting for transfers between devices  35.3 us
    all_gather x1, blocking collectives, local(): reports_group = lax.all_gather(reports_own, 'dp', axis=0, tiled=True)  32.2 us
    all_gather x1, blocking collectives, local(): lax.all_gather(both[0], ('section', 'tensor'), axis=0, tiled=True)  11.9 us
  transfers between devices with their start and end apart: 3, of which 2 were waited for; matrix products, arithmetic and copies ran while one was open for 1% of the time, Pallas kernels for 0%

commit v1 on v0

v1 whole, which is shorter than its diff:
```python
import functools

import jax
import jax.numpy as jnp
from jax import lax
from jax.experimental import pallas as pl
from jax.experimental.pallas import tpu as pltpu
from jax.sharding import PartitionSpec as P

MESH = pl.DeviceIdType.MESH
INNER = 2
UP_PARTS = 4
DOWN_PARTS = 2
X, Y, ZM, ZP, CORE = range(5)


def wait_bytes(ref, sem):
    pltpu.make_async_copy(ref, ref, sem).wait()


def kernel(
    dims,
    scale_ref, bias_ref, left_ref, tile_ref, x_ref, up_ref, down_ref,
    loss_out, slide_out, report_out,
    xs, up, down, hid, part, recv, emb, got, tiles, grad, grad_in, loss_acc, loss_row, loss_all,
    x_sem, up_sem, down_sem, part_send, part_recv, own_send, fwd_send, got_recv,
    tile_send, tile_recv, grad_send, grad_recv, loss_send, loss_recv,
):
    n_dp, n_section, n_tensor, n_part, n_rows, width, total = dims
    n_outer = n_dp // INNER
    quarter = xs.shape[0] // (n_section * n_tensor)
    own_rows = n_section * quarter
    d, s, x = lax.axis_index("dp"), lax.axis_index("section"), lax.axis_index("tensor")
    z, y = d // INNER, lax.rem(d, INNER)
    ox, oy, os = 1 - x, 1 - y, 1 - s
    n_all = n_dp * n_section * n_tensor
    me = (d * n_section + s) * n_tensor + x

    def device(zz, yy, ss, xx):
        return {"dp": zz * INNER + yy, "section": ss, "tensor": xx}

    def device_of(n):
        return {
            "dp": n // (n_section * n_tensor),
            "section": lax.rem(n // n_tensor, n_section),
            "tensor": lax.rem(n, n_tensor),
        }

    x_copies = []
    for half, t in ((0, ox), (1, x)):
        for q in range(n_section):
            x_copies.append(pltpu.make_async_copy(
                x_ref.at[pl.ds(pl.multiple_of((q * n_tensor + t) * quarter, 16), quarter)],
                xs.at[pl.ds(half * own_rows + q * quarter, quarter)],
                x_sem.at[half * n_section + q],
            ))
    for c in x_copies:
        c.start()
    up_w = up.shape[1] // UP_PARTS
    down_w = down.shape[1] // DOWN_PARTS

    def up_copy(i):
        cols = pl.ds(pl.multiple_of(i * up_w, 128), up_w)
        return pltpu.make_async_copy(up_ref.at[:, cols], up.at[:, cols], up_sem.at[i])

    def down_copy(i):
        cols = pl.ds(pl.multiple_of(i * down_w, 128), down_w)
        return pltpu.make_async_copy(down_ref.at[:, cols], down.at[:, cols], down_sem.at[i])

    for i in range(UP_PARTS):
        up_copy(i).start()
    for i in range(DOWN_PARTS):
        down_copy(i).start()

    barrier = pltpu.get_barrier_semaphore()

    def greet(n, carry):
        @pl.when(n != me)
        def _():
            pl.semaphore_signal(barrier, inc=1, device_id=device_of(n), device_id_type=MESH)
        return carry

    lax.fori_loop(0, n_all, greet, 0)
    grad[...] = jnp.zeros_like(grad)
    loss_acc[...] = jnp.zeros_like(loss_acc)
    tiles[d] = tile_ref[...]
    for c in x_copies:
        c.wait()

    def first(i, carry):
        up_copy(i).wait()
        cols = pl.ds(pl.multiple_of(i * up_w, 128), up_w)
        h = jnp.dot(xs[...], up[:, cols], preferred_element_type=jnp.float32)
        hid[:, cols] = jax.nn.gelu(h).astype(jnp.bfloat16)
        return carry

    lax.fori_loop(0, UP_PARTS, first, 0)

    def second(i, carry):
        down_copy(i).wait()
        cols = pl.ds(pl.multiple_of(i * down_w, 128), down_w)
        part[0, :, cols] = jnp.dot(
            hid[0:own_rows], down[:, cols], preferred_element_type=jnp.float32
        )
        return carry

    lax.fori_loop(0, DOWN_PARTS, second, 0)
    pl.semaphore_wait(barrier, n_all - 1)

    def part_copy(c):
        rows = pl.ds(c * n_rows, n_rows)
        return pltpu.make_async_remote_copy(
            part.at[0, rows], recv.at[rows], part_send.at[c], part_recv.at[c],
            device_id=device(z, y, s, ox), device_id_type=MESH,
        )

    for c in range(n_part):
        part_copy(c).start()

    def tile_copy(n):
        return pltpu.make_async_remote_copy(
            tile_ref, tiles.at[d], tile_send, tile_recv,
            device_id={"dp": n, "section": s, "tensor": x}, device_id_type=MESH,
        )

    def send_tile(n, carry):
        @pl.when(n != d)
        def _():
            tile_copy(n).start()
        return carry

    lax.fori_loop(0, n_dp, send_tile, 0)

    def second_own(i, carry):
        cols = pl.ds(pl.multiple_of(i * down_w, 128), down_w)
        part[1, :, cols] = jnp.dot(
            hid[own_rows:], down[:, cols], preferred_element_type=jnp.float32
        )
        return carry

    lax.fori_loop(0, DOWN_PARTS, second_own, 0)

    def slot(zz, yy, xx):
        return (zz * INNER + yy) * n_tensor + xx

    def place(c, sl):
        return got.at[c, pl.ds(pl.multiple_of(sl * n_rows, n_rows), n_rows)]

    def neighbour(way, ss):
        if way == X:
            return device(z, y, ss, ox)
        if way == Y:
            return device(z, oy, ss, x)
        if way == ZM:
            return device(z - 1, y, ss, x)
        if way == ZP:
            return device(z + 1, y, ss, x)
        return device(z, y, ss, x)

    def own_copy(c, way):
        sl = slot(z, y, x)
        return pltpu.make_async_remote_copy(
            emb.at[pl.ds(c * n_rows, n_rows)], place(c, sl), own_send.at[c, way],
            got_recv.at[c, sl], device_id=neighbour(way, os), device_id_type=MESH,
        )

    def fwd_copy(c, sl, way):
        return pltpu.make_async_remote_copy(
            place(c, sl), place(c, sl), fwd_send.at[c, sl, way], got_recv.at[c, sl],
            device_id=neighbour(way, s), device_id_type=MESH,
        )

    def guarded(way, act):
        if way == ZM:
            pl.when(z > 0)(act)
        elif way == ZP:
            pl.when(z < n_outer - 1)(act)
        else:
            act()

    def own_all(c, begin):
        for way in (ZM, ZP, Y, X, CORE):
            guarded(way, lambda: own_copy(c, way).start() if begin else own_copy(c, way).wait_send())

    def ways(c, rx, ry, far, side):
        onward = ZM if side > 0 else ZP
        if c == 0:
            if far:
                return (onward,)
            return (ZM, ZP) if rx else ((ZM, ZP, X) if ry else ())
        if ry:
            return ()
        if rx:
            return (Y,)
        return (onward, X, Y) if far else ()

    def handle(c, rx, ry, begin, k=0, side=0):
        far = side != 0
        sz = z + side * k
        sl = slot(sz, oy if ry else y, ox if rx else x)

        def act():
            if begin:
                wait_bytes(place(c, sl), got_recv.at[c, sl])
            for way in ways(c, rx, ry, far, side):
                copy = fwd_copy(c, sl, way)
                guarded(way, copy.start if begin else copy.wait_send)

        if far:
            pl.when((sz >= 0) & (sz < n_outer))(act)
        else:
            act()

    def far_loop(begin, blocks):
        def body(k, carry):
            for c, rx, ry in blocks:
                for side in (-1, 1):
                    handle(c, rx, ry, begin, k, side)
            return carry
        lax.fori_loop(1, n_outer, body, 0)

    def produce(c):
        rows = pl.ds(c * n_rows, n_rows)
        part_copy(c).wait_recv()
        raw = (part[1, rows] + recv[rows]) + xs[
            pl.ds(own_rows + c * n_rows, n_rows)
        ].astype(jnp.float32)
        norms = lax.rsqrt(jnp.sum(raw * raw, axis=-1, keepdims=True) + 1e-06)
        emb[rows] = (raw * norms).astype(jnp.bfloat16)
        own_all(c, True)

    others = range(1, n_part)
    near_z = [(c, 0, 0) for c in others] + [(0, 0, 0), (0, 0, 1)]
    far_z = [(0, 1, 0), (0, 1, 1)] + [(c, 1, 0) for c in others]
    scale_value, bias_value = scale_ref[0], bias_ref[0]

    def score(c):
        group = INNER * n_tensor * n_rows

        def body(g, carry):
            block = got[c, pl.ds(pl.multiple_of(g * group, group), group)]
            logits = scale_value * lax.dot_general(
                emb[...], block, (((1,), (1,)), ((), ())), preferred_element_type=jnp.float32
            ) + bias_value
            ids = tiles[g * INNER, c:c + 1]
            for i in range(1, INNER):
                ids = ids + tiles[g * INNER + i, c:c + 1]
            sign = jnp.where(left_ref[...] == ids, 1.0, -1.0).astype(jnp.float32)
            u = -sign * logits
            e = jnp.exp(-jnp.abs(u))
            loss_acc[...] += jnp.maximum(u, 0.0) + jnp.log1p(e)
            sigmoid = jnp.where(u >= 0, 1.0, e) / (1.0 + e)
            weight = (-scale_value * sign * sigmoid).astype(jnp.bfloat16)
            grad[...] += jnp.dot(weight, block, preferred_element_type=jnp.float32)
            return carry

        lax.fori_loop(0, n_outer, body, 0)

    produce(0)
    handle(0, 0, 1, True)
    for c in others:
        produce(c)
    far_loop(True, near_z)
    handle(0, 1, 0, True)
    handle(0, 1, 1, True)
    for c in others:
        handle(c, 1, 0, True)
    far_loop(True, far_z)
    for c in range(n_part):
        handle(c, 0, 0, True)
    wait_bytes(tiles.at[pl.ds(0, n_dp - 1)], tile_recv)
    score(0)
    for c in others:
        handle(c, 0, 1, True)
        handle(c, 1, 1, True)
        far_loop(True, [(c, 0, 1), (c, 1, 1)])
        score(c)

    grad_copy = pltpu.make_async_remote_copy(
        grad.at[pl.ds(pl.multiple_of(os * quarter, 16), quarter)], grad_in, grad_send, grad_recv,
        device_id=device(z, y, os, x), device_id_type=MESH,
    )
    grad_copy.start()
    loss_row[...] = jnp.sum(loss_acc[...], axis=0, keepdims=True)
    loss_all[me] = loss_row[...]

    def loss_copy(n):
        return pltpu.make_async_remote_copy(
            loss_row, loss_all.at[me], loss_send, loss_recv,
            device_id=device_of(n), device_id_type=MESH,
        )

    def send_loss(n, carry):
        @pl.when(n != me)
        def _():
            loss_copy(n).start()
        return carry

    lax.fori_loop(0, n_all, send_loss, 0)

    for c in range(n_part):
        part_copy(c).wait_send()
        own_all(c, False)
    wait_bytes(tiles.at[pl.ds(0, n_dp - 1)], tile_send)
    handle(0, 0, 1, False)
    handle(0, 1, 0, False)
    handle(0, 1, 1, False)
    for c in others:
        handle(c, 1, 0, False)
    far_loop(False, near_z)
    far_loop(False, far_z)

    mine = grad[pl.ds(pl.multiple_of(s * quarter, 16), quarter)]
    grad_copy.wait()

    @pl.when(s == 0)
    def _():
        slide_out[...] = mine
        report_out[...] = grad_in[...]

    @pl.when(s != 0)
    def _():
        slide_out[...] = grad_in[...]
        report_out[...] = mine

    wait_bytes(loss_all.at[pl.ds(0, n_all - 1)], loss_send)
    wait_bytes(loss_all.at[pl.ds(0, n_all - 1)], loss_recv)
    loss_out[0] = jnp.sum(loss_all[...]) * (0.5 / total)


def local(tower_input, up_weight, down_weight, pair, scale, bias):
    n_dp = lax.axis_size("dp")
    n_section = lax.axis_size("section")
    n_tensor = lax.axis_size("tensor")
    d, s, x = lax.axis_index("dp"), lax.axis_index("section"), lax.axis_index("tensor")
    inputs, up_w, down_w = tower_input[0], up_weight[0], down_weight[0]
    rows, width = inputs.shape
    hidden = up_w.shape[1]
    group = n_section * n_tensor
    quarter = rows // group
    own_rows = n_section * quarter
    total = n_dp * rows
    n_rows = 128 // (INNER * n_tensor)
    n_part = own_rows // n_rows
    chips = n_dp * n_tensor

    ids = d * rows + jnp.arange(rows, dtype=jnp.int32)
    left = jnp.where(s == 0, pair, ids).reshape(n_section, n_tensor, quarter)
    left = lax.dynamic_index_in_dim(left, x, 1, keepdims=False).reshape(own_rows, 1)
    left = jnp.broadcast_to(left, (own_rows, 128))
    right = jnp.where(s == 0, ids, pair).reshape(n_section, n_tensor, quarter)
    right = right.transpose(1, 0, 2).reshape(n_tensor, n_part, n_rows)
    right = right.transpose(1, 0, 2).reshape(n_part, 1, n_tensor * n_rows)
    here = jnp.arange(INNER, dtype=jnp.int32)[None, :, None] == lax.rem(d, INNER)
    tile = jnp.where(here, right, 0).reshape(n_part, 128)
    tile = jnp.pad(tile, ((0, 8 - n_part), (0, 0)))

    f32, bf16 = jnp.float32, jnp.bfloat16
    vmem = pl.BlockSpec(memory_space=pltpu.VMEM)
    smem = pl.BlockSpec(memory_space=pltpu.SMEM)
    hbm = pl.BlockSpec(memory_space=pl.ANY)
    dma = pltpu.SemaphoreType.DMA
    n_all = n_dp * group
    dims = (n_dp, n_section, n_tensor, n_part, n_rows, width, total)
    return pl.pallas_call(
        functools.partial(kernel, dims),
        out_shape=(
            jax.ShapeDtypeStruct((1,), f32),
            jax.ShapeDtypeStruct((quarter, width), f32),
            jax.ShapeDtypeStruct((quarter, width), f32),
        ),
        in_specs=[smem, smem, vmem, vmem, hbm, hbm, hbm],
        out_specs=(smem, vmem, vmem),
        scratch_shapes=[
            pltpu.VMEM((rows, width), bf16),
            pltpu.VMEM((width, hidden), bf16),
            pltpu.VMEM((hidden, width), bf16),
            pltpu.VMEM((rows, hidden), bf16),
            pltpu.VMEM((2, own_rows, width), f32),
            pltpu.VMEM((own_rows, width), f32),
            pltpu.VMEM((own_rows, width), bf16),
            pltpu.VMEM((n_part, chips * n_rows, width), bf16),
            pltpu.VMEM((n_dp, 8, 128), jnp.int32),
            pltpu.VMEM((own_rows, width), f32),
            pltpu.VMEM((quarter, width), f32),
            pltpu.VMEM((own_rows, 128), f32),
            pltpu.VMEM((1, 128), f32),
            pltpu.VMEM((n_all, 1, 128), f32),
            dma((group,)),
            dma((UP_PARTS,)),
            dma((DOWN_PARTS,)),
            dma((n_part,)),
            dma((n_part,)),
            dma((n_part, 5)),
            dma((n_part, chips, 4)),
            dma((n_part, chips)),
            dma, dma, dma, dma, dma, dma,
        ],
        compiler_params=pltpu.CompilerParams(
            collective_id=0, has_side_effects=True, vmem_limit_bytes=60 * 1024 * 1024
        ),
    )(scale, bias, left, tile, inputs, up_w, down_w)


def solution(mesh):
    return jax.shard_map(
        local,
        mesh=mesh,
        in_specs=(
            P("section", "dp", None),
            P("section", None, "tensor"),
            P("section", "tensor", None),
            P("dp"),
            P(),
            P(),
        ),
        out_specs=(P(), P(("dp", "section", "tensor"), None), P(("dp", "section", "tensor"), None)),
        check_vma=False,
    )
```

time: 207 us -> 71.6 us (0.35)
  blocking collectives: 86.5 us -> 0 us
  waiting for transfers between devices: 85.6 us -> 0 us
  Pallas kernels: 0 us -> 61.7 us
  between operations: 18.1 us -> 3.71 us
  matrix products: 10.6 us -> 0 us
  local copies, waits for them, and re-layouts: 0.69 us -> 5.24 us
  other arithmetic: 4.52 us -> 0.7 us
    pallas_call x0 -> x1, Pallas kernels: none -> 61.7 us  [local(): pl.pallas_call(functools.partial(kernel, dims), out_shape=(jax.ShapeDtype...]
    reduce_scatter x2 -> x0, waiting for transfers between devices: 50.3 us -> none  [the longest x1 50.3 us: local(): lax.psum_scatter(report_top + report_bottom, 'dp', scatter_dimension=0, t...]
    all_gather x2 -> x0, blocking collectives: 44.1 us -> none  [the longest x1 32.2 us: local(): reports_group = lax.all_gather(reports_own, 'dp', axis=0, tiled=True)]
    psum x1 -> x0, blocking collectives: 38.5 us -> none  [local(): loss = lax.psum(loss_sum, ('dp', 'section', 'tensor')) / total]
    unnamed x4 -> x0, waiting for transfers between devices: 35.3 us -> none
    dot_general x8 -> x0, matrix products: 10.6 us -> none  [the longest x1 3.79 us: local(): jnp.dot(inputs, up_weight[0], preferred_element_type=jnp.float32)]
    all_to_all x1 -> x0, blocking collectives: 3.89 us -> none  [local(): lax.all_to_all(embedded, 'section', split_axis=0, concat_axis=0, tiled=True)]
    unnamed x9 -> x2, local copies, waits for them, and re-layouts: 0.61 us -> 3.23 us
  transfers between devices with their start and end apart: 3 -> 0, of which waited for: 2 -> 0; matrix products, arithmetic and copies ran while one was open for 1% -> 0% of each run, Pallas kernels for 0% -> 0%
where the time goes in v1:
time: 71.6 us; the launch traced here: 71.4 us
  Pallas kernels  61.7 us (86%)
  local copies, waits for them, and re-layouts  5.24 us (7%)
  between operations  3.71 us (5%)
    pallas_call x1, Pallas kernels, local(): pl.pallas_call(functools.partial(kernel, dims), out_shape=(jax.ShapeDtype...  61.7 us
    unnamed x2, local copies, waits for them, and re-layouts  3.23 us

profile of v1, /device:TPU:0, one launch (start us, length us, event | category | flops | bytes accessed | tf_op | source)
XLA Modules:
  0.0 71.4 jit_solution(7223959062259686847)
XLA Ops:
  1.9 0.1 broadcast_in_dim.38
  2.0 0.1 broadcast_in_dim.39
  2.1 0.7 fusion
  2.8 0.1 reshape.29
  2.9 0.1 reshape.30
  3.0 0.1 broadcast_in_dim.41
  3.1 0.1 broadcast_in_dim.43
  3.2 0.6 pad.4.tile_ref
  3.8 0.1 reshape.28
  3.9 0.1 broadcast_in_dim.36
  3.9 0.7 broadcast_in_dim.37.left_ref
  4.7 61.7 %shard_map.85 = (f32[1]{0:T(128)}, f32[48,1024]{1,0:T(8,128)}, f32[48,1024]{1,0:T(8,128)}) custom-call(f32[1]{0:T(128)S(6)} %copy.14.scale_ref, f32[1]{0:T(128)S(6)} %copy.15.bias_ref, s32[96,128]{1,0:T(8,128)} %broadcast_in_dim.37.left_ref, s32[8,128]{1,0:T(8,128)} %pad.4.tile_ref, bf16[192,1024]{1,0:T(8,128)(2,1)} %bitcast.7, bf16[1024,2048]{1,0:T(8,128)(2,1)} %bitcast.5, ...), custom_call_target="tpu_custom_call" | custom-call | tf_op jit(solution)/shard_map/pallas_call | solution.py:365
  67.0 1.6 %copy.17 = f32[48,1024]{1,0:T(8,128)} copy(f32[48,1024]{1,0:T(8,128)} %get-tuple-element.9) | data formatting | bytes 393216
  68.6 1.6 %copy.18 = f32[48,1024]{1,0:T(8,128)} copy(f32[48,1024]{1,0:T(8,128)} %get-tuple-element.10) | data formatting | bytes 393216
  (6 shorter events, 0.1 us)

commit v2 on v1

v2 whole, which is shorter than its diff:
```python
import functools
import math

import jax
import jax.numpy as jnp
from jax import lax
from jax.experimental import pallas as pl
from jax.experimental.pallas import tpu as pltpu
from jax.sharding import PartitionSpec as P

MESH = pl.DeviceIdType.MESH
INNER = 2
UP_PARTS = 4
DOWN_PARTS = 2
X, Y, ZM, ZP, CORE = range(5)
ROUTES = ("zxy", "zxy", "zyx", "yxz", "xzy", "zyx")
N_SUB = len(ROUTES)
ORDER = (
    (0, 0, 0, 0), (1, 0, 0, 0), (0, 0, 0, 1), (2, 0, 0, 0),
    (1, 0, 0, 1), (3, 0, 0, 0), (0, 0, 0, 2), (2, 0, 0, 1),
    (4, 0, 0, 0), (2, 0, 1, 0), (1, 0, 0, 2), (3, 0, 0, 1),
    (5, 0, 0, 0), (0, 1, 0, 0), (3, 0, 1, 0), (0, 0, 0, 3),
    (4, 0, 0, 1), (1, 1, 0, 0), (2, 0, 0, 2), (0, 1, 0, 1),
    (1, 0, 0, 3), (5, 0, 0, 1), (2, 0, 1, 1), (3, 0, 0, 2),
    (1, 1, 0, 1), (3, 0, 1, 1), (5, 0, 1, 0), (3, 1, 0, 0),
    (4, 0, 0, 2), (2, 0, 0, 3), (0, 1, 0, 2), (5, 0, 0, 2),
    (4, 1, 0, 0), (3, 0, 0, 3), (3, 0, 1, 2), (2, 0, 1, 2),
    (1, 1, 0, 2), (4, 0, 0, 3), (3, 1, 0, 1), (0, 1, 0, 3),
    (5, 0, 0, 3), (4, 1, 0, 1), (3, 1, 1, 0), (5, 0, 1, 1),
    (3, 1, 0, 2), (2, 0, 1, 3), (3, 0, 1, 3), (1, 1, 0, 3),
    (4, 1, 0, 2), (3, 1, 0, 3), (3, 1, 1, 1), (5, 0, 1, 2),
    (4, 1, 0, 3), (3, 1, 1, 2), (5, 0, 1, 3), (3, 1, 1, 3),
)


def wait_bytes(ref, sem):
    pltpu.make_async_copy(ref, ref, sem).wait()


def kernel(
    dims,
    scale_ref, bias_ref, pair_ref, x_ref, up_ref, down_ref,
    loss_out, mine_out, theirs_out,
    xs, up, down, hid, part, recv, emb, got, left, tile, tiles, scores, grad, loss_acc, loss_row, loss_all,
    x_sem, up_sem, down_sem, part_send, part_recv, own_send, near_send, fwd_send, got_recv,
    tile_send, tile_recv, grad_send, grad_recv, loss_send, loss_recv,
):
    n_dp, n_section, n_tensor, n_part, n_rows, width, total = dims
    n_outer = n_dp // INNER
    quarter = xs.shape[0] // (n_section * n_tensor)
    own_rows = n_section * quarter
    d, s, x = lax.axis_index("dp"), lax.axis_index("section"), lax.axis_index("tensor")
    z, y = d // INNER, lax.rem(d, INNER)
    ox, oy, os = 1 - x, 1 - y, 1 - s
    n_all = n_dp * n_section * n_tensor
    me = (d * n_section + s) * n_tensor + x

    def device(zz, yy, ss, xx):
        return {"dp": zz * INNER + yy, "section": ss, "tensor": xx}

    def device_of(n):
        return {
            "dp": n // (n_section * n_tensor),
            "section": lax.rem(n // n_tensor, n_section),
            "tensor": lax.rem(n, n_tensor),
        }

    n_sub_rows = own_rows // N_SUB

    def step_of(value, size, count):
        return sum((value >= i * size).astype(jnp.int32) for i in range(1, count))

    def make_ids():
        rows = n_section * n_tensor * quarter
        iota = lambda shape, dim: lax.broadcasted_iota(jnp.int32, shape, dim)
        pair = pair_ref[...].astype(jnp.float32)
        ids = (d * rows + iota((1, rows), 1)).astype(jnp.float32)
        first_core = jnp.broadcast_to(s, (1, rows)) == 0

        def natural(row, t):
            q = step_of(row, quarter, n_section)
            return (q * n_tensor + t) * quarter + (row - q * quarter)

        hit = iota((own_rows, rows), 1) == natural(iota((own_rows, rows), 0), x)
        kept = jnp.sum(jnp.where(hit, jnp.where(first_core, pair, ids), 0.0), axis=1, keepdims=True)
        left[...] = jnp.broadcast_to(kept, (own_rows, 128)).astype(jnp.int32)
        hit = iota((rows, rows), 0) == iota((rows, rows), 1)
        column = jnp.sum(jnp.where(hit, jnp.where(first_core, ids, pair), 0.0), axis=1, keepdims=True)
        lane = iota((rows, 128), 1)
        inner = step_of(lane, n_tensor * n_rows, INNER)
        lane = lane - inner * (n_tensor * n_rows)
        t = step_of(lane, n_rows, n_tensor)
        for c in range(n_part):
            hit = iota((rows, 128), 0) == natural(lane - t * n_rows + c * n_rows, t)
            line = jnp.sum(jnp.where(hit & (inner == y), column, 0.0), axis=0, keepdims=True)
            tile[c:c + 1] = line.astype(jnp.int32)
        tiles[d] = tile[...]

    x_copies = []
    for half, t in ((0, ox), (1, x)):
        for q in range(n_section):
            x_copies.append(pltpu.make_async_copy(
                x_ref.at[pl.ds(pl.multiple_of((q * n_tensor + t) * quarter, 16), quarter)],
                xs.at[pl.ds(half * own_rows + q * quarter, quarter)],
                x_sem.at[half * n_section + q],
            ))
    for c in x_copies:
        c.start()
    up_w = up.shape[1] // UP_PARTS
    down_w = down.shape[1] // DOWN_PARTS

    def up_copy(i):
        cols = pl.ds(pl.multiple_of(i * up_w, 128), up_w)
        return pltpu.make_async_copy(up_ref.at[:, cols], up.at[:, cols], up_sem.at[i])

    def down_copy(i):
        cols = pl.ds(pl.multiple_of(i * down_w, 128), down_w)
        return pltpu.make_async_copy(down_ref.at[:, cols], down.at[:, cols], down_sem.at[i])

    for i in range(UP_PARTS):
        up_copy(i).start()
    for i in range(DOWN_PARTS):
        down_copy(i).start()

    barrier = pltpu.get_barrier_semaphore()

    def greet(n, carry):
        @pl.when(n != me)
        def _():
            pl.semaphore_signal(barrier, inc=1, device_id=device_of(n), device_id_type=MESH)
        return carry

    lax.fori_loop(0, n_all, greet, 0)
    grad[...] = jnp.zeros_like(grad)
    loss_acc[...] = jnp.zeros_like(loss_acc)
    make_ids()
    for c in x_copies:
        c.wait()

    def first(i, carry):
        up_copy(i).wait()
        cols = pl.ds(pl.multiple_of(i * up_w, 128), up_w)
        h = jnp.dot(xs[...], up[:, cols], preferred_element_type=jnp.float32)
        hid[:, cols] = jax.nn.gelu(h).astype(jnp.bfloat16)
        return carry

    lax.fori_loop(0, UP_PARTS, first, 0)

    def second(i, carry):
        down_copy(i).wait()
        cols = pl.ds(pl.multiple_of(i * down_w, 128), down_w)
        part[0, :, cols] = jnp.dot(
            hid[0:own_rows], down[:, cols], preferred_element_type=jnp.float32
        )
        return carry

    lax.fori_loop(0, DOWN_PARTS, second, 0)
    pl.semaphore_wait(barrier, n_all - 1)

    def part_copy(c):
        rows = pl.ds(c * n_sub_rows, n_sub_rows)
        return pltpu.make_async_remote_copy(
            part.at[0, rows], recv.at[rows], part_send.at[c], part_recv.at[c],
            device_id=device(z, y, s, ox), device_id_type=MESH,
        )

    for c in range(N_SUB):
        part_copy(c).start()

    def tile_copy(n):
        return pltpu.make_async_remote_copy(
            tile, tiles.at[d], tile_send, tile_recv,
            device_id={"dp": n, "section": s, "tensor": x}, device_id_type=MESH,
        )

    def send_tile(n, carry):
        @pl.when(n != d)
        def _():
            tile_copy(n).start()
        return carry

    lax.fori_loop(0, n_dp, send_tile, 0)

    def second_own(i, carry):
        cols = pl.ds(pl.multiple_of(i * down_w, 128), down_w)
        part[1, :, cols] = jnp.dot(
            hid[own_rows:], down[:, cols], preferred_element_type=jnp.float32
        )
        return carry

    lax.fori_loop(0, DOWN_PARTS, second_own, 0)

    def slot(zz, yy, xx):
        return (zz * INNER + yy) * n_tensor + xx

    def place(c, sl):
        per = n_rows // n_sub_rows
        start = pl.multiple_of(sl * n_rows + c % per * n_sub_rows, n_sub_rows)
        return got.at[c // per, pl.ds(start, n_sub_rows)]

    def neighbour(way, ss):
        if way == X:
            return device(z, y, ss, ox)
        if way == Y:
            return device(z, oy, ss, x)
        if way == ZM:
            return device(z - 1, y, ss, x)
        if way == ZP:
            return device(z + 1, y, ss, x)
        return device(z, y, ss, x)

    def own_copy(c, way):
        sl = slot(z, y, x)
        return pltpu.make_async_remote_copy(
            emb.at[pl.ds(c * n_sub_rows, n_sub_rows)], place(c, sl), own_send.at[c, way],
            got_recv.at[c, sl], device_id=neighbour(way, os), device_id_type=MESH,
        )

    def fwd_copy(c, sl, way, sem):
        return pltpu.make_async_remote_copy(
            place(c, sl), place(c, sl), sem, got_recv.at[c, sl],
            device_id=neighbour(way, s), device_id_type=MESH,
        )

    def guarded(way, act):
        if way == ZM:
            pl.when(z > 0)(act)
        elif way == ZP:
            pl.when(z < n_outer - 1)(act)
        else:
            act()

    def own_all(c, begin):
        for way in (ZM, ZP, Y, X, CORE):
            guarded(way, lambda: own_copy(c, way).start() if begin else own_copy(c, way).wait_send())

    def ways(c, rx, ry, far, side):
        moved = {"x": rx, "y": ry, "z": far}
        route = ROUTES[c]
        done = max((i + 1 for i in range(3) if moved[route[i]]), default=0)
        if not done:
            return ()
        out = {"x": (X,), "y": (Y,), "z": (ZM, ZP)}
        onward = (ZM if side > 0 else ZP,) if route[done - 1] == "z" else ()
        return sum((out[i] for i in route[done:]), onward)

    def handle(c, rx, ry, begin, k=0, side=0):
        far = side != 0
        sz = z + side * k
        sl = slot(sz, oy if ry else y, ox if rx else x)

        def act():
            if begin:
                wait_bytes(place(c, sl), got_recv.at[c, sl])
            for way in ways(c, rx, ry, far, side):
                if way == ZP and not far:
                    sem = near_send.at[c, rx * INNER + ry]
                else:
                    sem = fwd_send.at[c, sl, min(way, ZM)]
                copy = fwd_copy(c, sl, way, sem)
                guarded(way, copy.start if begin else copy.wait_send)

        if far:
            pl.when((sz >= 0) & (sz < n_outer))(act)
        else:
            act()

    def far_loop(begin, blocks):
        def body(k, carry):
            for c, rx, ry in blocks:
                for side in (-1, 1):
                    handle(c, rx, ry, begin, k, side)
            return carry
        lax.fori_loop(1, n_outer, body, 0)

    def produce(c):
        rows = pl.ds(c * n_sub_rows, n_sub_rows)
        part_copy(c).wait_recv()
        raw = (part[1, rows] + recv[rows]) + xs[
            pl.ds(own_rows + c * n_sub_rows, n_sub_rows)
        ].astype(jnp.float32)
        norms = lax.rsqrt(jnp.sum(raw * raw, axis=-1, keepdims=True) + 1e-06)
        emb[rows] = (raw * norms).astype(jnp.bfloat16)
        own_all(c, True)

    scale_value, bias_value = scale_ref[0], bias_ref[0]
    batch = math.gcd(4, n_outer)
    group = batch * INNER * n_tensor * n_rows
    group_lanes = lambda g: pl.ds(pl.multiple_of(g * group, 128), group)

    def score(c):
        def body(g, carry):
            block = got[c, pl.ds(pl.multiple_of(g * group, group), group)]
            logits = scale_value * lax.dot_general(
                emb[...], block, (((1,), (1,)), ((), ())), preferred_element_type=jnp.float32
            ) + bias_value
            lines = []
            for j in range(batch):
                at = (g * batch + j) * INNER
                lines.append(sum(tiles[at + i, c:c + 1] for i in range(INNER)))
            for j in range(batch):
                sign = jnp.where(left[...] == lines[j], 1.0, -1.0).astype(jnp.float32)
                u = -sign * logits[:, j * 128:(j + 1) * 128]
                e = jnp.exp(-jnp.abs(u))
                loss_acc[...] += jnp.maximum(u, 0.0) + jnp.log1p(e)
                sigmoid = jnp.where(u >= 0, 1.0, e) / (1.0 + e)
                lanes = pl.ds(pl.multiple_of(g * group + j * 128, 128), 128)
                scores[:, lanes] = (-scale_value * sign * sigmoid).astype(jnp.bfloat16)
            return carry

        lax.fori_loop(0, n_outer // batch, body, 0)

    def collect(c):
        def body(g, carry):
            block = got[c, pl.ds(pl.multiple_of(g * group, group), group)]
            grad[...] += jnp.dot(
                scores[:, group_lanes(g)], block, preferred_element_type=jnp.float32
            )
            return carry

        lax.fori_loop(0, n_outer // batch, body, 0)

    shifts = [(c, rx, ry) for c in range(N_SUB) for rx in (0, 1) for ry in (0, 1)]
    passed = [b for b in sorted(shifts, key=lambda b: b[1] + b[2]) if ways(*b, True, 1)]
    table_k = max(k for _, _, _, k in ORDER)

    def pass_on(begin):
        for c, rx, ry, k in ORDER:
            if k >= n_outer:
                continue
            if k:
                for side in (-1, 1):
                    handle(c, rx, ry, begin, k, side)
            elif rx or ry:
                handle(c, rx, ry, begin)
            elif begin:
                produce(c)
            else:
                own_all(c, False)

        def body(k, carry):
            for c, rx, ry in passed:
                for side in (-1, 1):
                    handle(c, rx, ry, begin, k, side)
            return carry

        if table_k + 1 < n_outer:
            lax.fori_loop(table_k + 1, n_outer, body, 0)

    def finish(c):
        per = n_rows // n_sub_rows
        blocks = [b for b in shifts if b[0] // per == c]
        for b in blocks:
            if b[1:] == (0, 0) or not ways(*b, False, 0):
                handle(*b, True)
        ends = [b for b in blocks if not ways(*b, True, 1)]

        def body(k, carry):
            for b in ends:
                for side in (-1, 1):
                    handle(*b, True, k, side)
            return carry

        lax.fori_loop(1, n_outer, body, 0)

    pass_on(True)
    wait_bytes(tiles.at[pl.ds(0, n_dp - 1)], tile_recv)

    def loss_copy(n):
        return pltpu.make_async_remote_copy(
            loss_row, loss_all.at[me], loss_send, loss_recv,
            device_id=device_of(n), device_id_type=MESH,
        )

    def send_loss(n, carry):
        @pl.when(n != me)
        def _():
            loss_copy(n).start()
        return carry

    for c in range(n_part):
        finish(c)
        score(c)
        if c == n_part - 1:
            loss_row[...] = jnp.sum(loss_acc[...], axis=0, keepdims=True)
            loss_all[me] = loss_row[...]
            lax.fori_loop(0, n_all, send_loss, 0)
        collect(c)

    grad_copy = pltpu.make_async_remote_copy(
        grad.at[pl.ds(pl.multiple_of(os * quarter, 16), quarter)], theirs_out, grad_send, grad_recv,
        device_id=device(z, y, os, x), device_id_type=MESH,
    )
    grad_copy.start()
    mine_out[...] = grad[pl.ds(pl.multiple_of(s * quarter, 16), quarter)]
    for c in range(N_SUB):
        part_copy(c).wait_send()
    wait_bytes(tiles.at[pl.ds(0, n_dp - 1)], tile_send)
    pass_on(False)
    grad_copy.wait()
    wait_bytes(loss_all.at[pl.ds(0, n_all - 1)], loss_send)
    wait_bytes(loss_all.at[pl.ds(0, n_all - 1)], loss_recv)
    loss_out[0] = jnp.sum(loss_all[...]) * (0.5 / total)


def local(tower_input, up_weight, down_weight, pair, scale, bias):
    n_dp = lax.axis_size("dp")
    n_section = lax.axis_size("section")
    n_tensor = lax.axis_size("tensor")
    inputs, up_w, down_w = tower_input[0], up_weight[0], down_weight[0]
    rows, width = inputs.shape
    hidden = up_w.shape[1]
    group = n_section * n_tensor
    quarter = rows // group
    own_rows = n_section * quarter
    total = n_dp * rows
    n_rows = 128 // (INNER * n_tensor)
    n_part = own_rows // n_rows
    chips = n_dp * n_tensor

    f32, bf16 = jnp.float32, jnp.bfloat16
    vmem = pl.BlockSpec(memory_space=pltpu.VMEM)
    smem = pl.BlockSpec(memory_space=pltpu.SMEM)
    hbm = pl.BlockSpec(memory_space=pl.ANY)
    dma = pltpu.SemaphoreType.DMA
    n_all = n_dp * group
    dims = (n_dp, n_section, n_tensor, n_part, n_rows, width, total)
    loss, mine, theirs = pl.pallas_call(
        functools.partial(kernel, dims),
        out_shape=(
            jax.ShapeDtypeStruct((1,), f32),
            jax.ShapeDtypeStruct((quarter, width), f32),
            jax.ShapeDtypeStruct((quarter, width), f32),
        ),
        in_specs=[smem, smem, vmem, hbm, hbm, hbm],
        out_specs=(smem, vmem, vmem),
        scratch_shapes=[
            pltpu.VMEM((rows, width), bf16),
            pltpu.VMEM((width, hidden), bf16),
            pltpu.VMEM((hidden, width), bf16),
            pltpu.VMEM((rows, hidden), bf16),
            pltpu.VMEM((2, own_rows, width), f32),
            pltpu.VMEM((own_rows, width), f32),
            pltpu.VMEM((own_rows, width), bf16),
            pltpu.VMEM((n_part, chips * n_rows, width), bf16),
            pltpu.VMEM((own_rows, 128), jnp.int32),
            pltpu.VMEM((8, 128), jnp.int32),
            pltpu.VMEM((n_dp, 8, 128), jnp.int32),
            pltpu.VMEM((own_rows, chips * n_rows), bf16),
            pltpu.VMEM((own_rows, width), f32),
            pltpu.VMEM((own_rows, 128), f32),
            pltpu.VMEM((1, 128), f32),
            pltpu.VMEM((n_all, 1, 128), f32),
            dma((group,)),
            dma((UP_PARTS,)),
            dma((DOWN_PARTS,)),
            dma((N_SUB,)),
            dma((N_SUB,)),
            dma((N_SUB, 5)),
            dma((N_SUB, n_tensor * INNER)),
            dma((N_SUB, chips, 3)),
            dma((N_SUB, chips)),
            dma, dma, dma, dma, dma, dma,
        ],
        compiler_params=pltpu.CompilerParams(
            collective_id=0, has_side_effects=True, vmem_limit_bytes=60 * 1024 * 1024
        ),
    )(scale, bias, pair.reshape(1, rows), inputs, up_w, down_w)
    first_core = lax.axis_index("section") == 0
    return (
        loss,
        jnp.where(first_core, mine, theirs),
        jnp.where(first_core, theirs, mine),
    )


def solution(mesh):
    return jax.shard_map(
        local,
        mesh=mesh,
        in_specs=(
            P("section", "dp", None),
            P("section", None, "tensor"),
            P("section", "tensor", None),
            P("dp"),
            P(),
            P(),
        ),
        out_specs=(P(), P(("dp", "section", "tensor"), None), P(("dp", "section", "tensor"), None)),
        check_vma=False,
    )
```

time: 71.6 us -> 59.1 us (0.83)
  Pallas kernels: 61.7 us -> 53.4 us
  local copies, waits for them, and re-layouts: 5.24 us -> 0 us
  other arithmetic: 0.7 us -> 1.8 us
    pallas_call x1, Pallas kernels: 61.7 us -> 53.4 us  [local(): pl.pallas_call(functools.partial(kernel, dims), out_shape=(jax.ShapeDtype...]
    unnamed x2 -> x0, local copies, waits for them, and re-layouts: 3.23 us -> none
    broadcast_in_dim x7 -> x0, local copies, waits for them, and re-layouts: 1.12 us -> none  [the longest x2 0.79 us: local(): left = jnp.broadcast_to(left, (own_rows, 128))]
    select_n x2 -> x1, other arithmetic: 0.69 us -> 1.8 us  [local(): jnp.where(first_core, theirs, mine)]
where the time goes in v2:
time: 59.1 us; the launch traced here: 58.9 us
  Pallas kernels  53.4 us (90%)
  between operations  3.76 us (6%)
  other arithmetic  1.8 us (3%)
    pallas_call x1, Pallas kernels, local(): pl.pallas_call(functools.partial(kernel, dims), out_shape=(jax.ShapeDtype...  53.4 us
    select_n x1, other arithmetic, local(): jnp.where(first_core, theirs, mine)  1.8 us

profile of v2, /device:TPU:0, one launch (start us, length us, event | category | flops | bytes accessed | tf_op | source)
XLA Modules:
  0.0 58.9 jit_solution(12544858317753291163)
XLA Ops:
  1.9 53.4 %shard_map.85 = (f32[1]{0:T(128)}, f32[48,1024]{1,0:T(8,128)}, f32[48,1024]{1,0:T(8,128)}) custom-call(f32[1]{0:T(128)S(6)} %copy.10.scale_ref, f32[1]{0:T(128)S(6)} %copy.11.bias_ref, s32[1,192]{1,0:T(1,128)} %bitcast.7, bf16[192,1024]{1,0:T(8,128)(2,1)} %bitcast.6, bf16[1024,2048]{1,0:T(8,128)(2,1)} %bitcast.4, bf16[2048,1024]{1,0:T(8,128)(2,1)} %bitcast.5), custom_call_target="tpu_custom_call" | custom-call | tf_op jit(solution)/shard_map/pallas_call | solution.py:428
  55.3 1.8 %broadcast_select_fusion = (f32[48,1024]{1,0:T(8,128)}, f32[48,1024]{1,0:T(8,128)}) fusion(f32[48,1024]{1,0:T(8,128)} %get-tuple-element.8, f32[48,1024]{1,0:T(8,128)} %get-tuple-element.7, pred[]{:T(512)S(6)} %eq.3), kind=kLoop, calls=%fused_computation | loop fusion | flops 98304 | bytes 786433 | tf_op jit(solution)/shard_map/jit(_where)/select_n | solution.py:473

commit v3 on v2

--- a/solution.py
+++ b/solution.py
@@ -137,14 +137,20 @@
     for c in x_copies:
         c.wait()
 
-    def first(i, carry):
-        up_copy(i).wait()
-        cols = pl.ds(pl.multiple_of(i * up_w, 128), up_w)
-        h = jnp.dot(xs[...], up[:, cols], preferred_element_type=jnp.float32)
-        hid[:, cols] = jax.nn.gelu(h).astype(jnp.bfloat16)
-        return carry
-
-    lax.fori_loop(0, UP_PARTS, first, 0)
+    def first(half):
+        rows = pl.ds(half * own_rows, own_rows)
+
+        def body(i, carry):
+            if half == 0:
+                up_copy(i).wait()
+            cols = pl.ds(pl.multiple_of(i * up_w, 128), up_w)
+            h = jnp.dot(xs[rows], up[:, cols], preferred_element_type=jnp.float32)
+            hid[rows, cols] = jax.nn.gelu(h).astype(jnp.bfloat16)
+            return carry
+
+        lax.fori_loop(0, UP_PARTS, body, 0)
+
+    first(0)
 
     def second(i, carry):
         down_copy(i).wait()
@@ -180,6 +186,8 @@
         return carry
 
     lax.fori_loop(0, n_dp, send_tile, 0)
+
+    first(1)
 
     def second_own(i, carry):
         cols = pl.ds(pl.multiple_of(i * down_w, 128), down_w)
@@ -368,14 +376,12 @@
 
     def loss_copy(n):
         return pltpu.make_async_remote_copy(
-            loss_row, loss_all.at[me], loss_send, loss_recv,
+            loss_row, loss_all.at[slot(z, y, x)], loss_send, loss_recv,
             device_id=device_of(n), device_id_type=MESH,
         )
 
     def send_loss(n, carry):
-        @pl.when(n != me)
-        def _():
-            loss_copy(n).start()
+        loss_copy(lax.rem(me + n, n_all)).start()
         return carry
 
     for c in range(n_part):
@@ -383,8 +389,12 @@
         score(c)
         if c == n_part - 1:
             loss_row[...] = jnp.sum(loss_acc[...], axis=0, keepdims=True)
-            loss_all[me] = loss_row[...]
-            lax.fori_loop(0, n_all, send_loss, 0)
+
+            @pl.when(s == 0)
+            def _():
+                loss_all[slot(z, y, x)] = loss_row[...]
+                lax.fori_loop(1, n_all, send_loss, 0)
+
         collect(c)
 
     grad_copy = pltpu.make_async_remote_copy(
@@ -398,9 +408,18 @@
     wait_bytes(tiles.at[pl.ds(0, n_dp - 1)], tile_send)
     pass_on(False)
     grad_copy.wait()
-    wait_bytes(loss_all.at[pl.ds(0, n_all - 1)], loss_send)
-    wait_bytes(loss_all.at[pl.ds(0, n_all - 1)], loss_recv)
-    loss_out[0] = jnp.sum(loss_all[...]) * (0.5 / total)
+    n_chips = n_dp * n_tensor
+
+    @pl.when(s == 0)
+    def _():
+        wait_bytes(loss_all.at[pl.ds(0, n_all - 1)], loss_send)
+        wait_bytes(loss_all.at[pl.ds(0, n_chips - 1)], loss_recv)
+
+    @pl.when(s != 0)
+    def _():
+        wait_bytes(loss_all.at[pl.ds(0, n_chips)], loss_recv)
+
+    loss_out[0] = jnp.sum(loss_all[0:n_chips]) / total
 
 
 def local(tower_input, up_weight, down_weight, pair, scale, bias):

time: 59.1 us -> 58.8 us (level)
  no operation moved by 1% of the time
where the time goes in v3:
time: 58.8 us; the launch traced here: 58.6 us
  Pallas kernels  53 us (90%)
  between operations  3.76 us (6%)
  other arithmetic  1.8 us (3%)
    pallas_call x1, Pallas kernels, local(): pl.pallas_call(functools.partial(kernel, dims), out_shape=(jax.ShapeDtype...  53 us
    select_n x1, other arithmetic, local(): jnp.where(first_core, theirs, mine)  1.8 us

profile of v3, /device:TPU:0, one launch (start us, length us, event | category | flops | bytes accessed | tf_op | source)
XLA Modules:
  0.0 58.6 jit_solution(5326817607732398827)
XLA Ops:
  1.9 53.0 %shard_map.85 = (f32[1]{0:T(128)}, f32[48,1024]{1,0:T(8,128)}, f32[48,1024]{1,0:T(8,128)}) custom-call(f32[1]{0:T(128)S(6)} %copy.10.scale_ref, f32[1]{0:T(128)S(6)} %copy.11.bias_ref, s32[1,192]{1,0:T(1,128)} %bitcast.7, bf16[192,1024]{1,0:T(8,128)(2,1)} %bitcast.6, bf16[1024,2048]{1,0:T(8,128)(2,1)} %bitcast.4, bf16[2048,1024]{1,0:T(8,128)(2,1)} %bitcast.5), custom_call_target="tpu_custom_call" | custom-call | tf_op jit(solution)/shard_map/pallas_call | solution.py:447
  55.0 1.8 %broadcast_select_fusion = (f32[48,1024]{1,0:T(8,128)}, f32[48,1024]{1,0:T(8,128)}) fusion(f32[48,1024]{1,0:T(8,128)} %get-tuple-element.8, f32[48,1024]{1,0:T(8,128)} %get-tuple-element.7, pred[]{:T(512)S(6)} %eq.3), kind=kLoop, calls=%fused_computation | loop fusion | flops 98304 | bytes 786433 | tf_op jit(solution)/shard_map/jit(_where)/select_n | solution.py:492
